TPU v7x, 32 devices: a whole 2x2x4 slice. The times are simulated.
32 devices in a mesh: gx: 4 (over z), gy: 8 (over y, x, core).
Axes of the slice: x: 2, y: 2, z: 4, core: 2. Of those that a mesh axis runs over, the one named last changes fastest.
Arguments:
- features: bfloat16 [40960, 2048], P(('gx', 'gy')), may hold values from -6 to 6
- counts: int32 [32], P(('gx', 'gy')), may hold values from 128 to 1280, as said below
- ref_mean: float32 [2048], replicated, may hold values from -6 to 6
- ref_root: float32 [2048, 2048], P('gx', 'gy'), as said below
Outputs:
- mean: float32 [2048], replicated
- root: float32 [2048, 2048], P('gx', 'gy')
- distance: float32 [], replicated
Inputs may be any that keep to these rules, and one draw needn't show every extreme that they name: Entry b counts the valid rows of shard b, which come first in it; a multiple of 128; some shard is full in every draw. `ref_root`: symmetric and positive definite.
All inputs are finite; a program needn't handle non-finite values.
Results may differ from a plain program's by a relative error of at most 0.0015.
The roundings to bfloat16 on the way count: a program that leaves them out, or rounds other values in their place, can miss the bound.
Values may be sent and summed in bfloat16 or wider, within the bound.
A program may use at most 128 MiB of HBM per device.

v0:
```python
import jax
import jax.numpy as jnp
from jax import lax
from jax.sharding import PartitionSpec as P

ITERS = 4


def product(left, right):
    left_half = left.astype(jnp.bfloat16)
    right_half = right.astype(jnp.bfloat16)
    panel = lax.all_gather(left_half, "gy", axis=1, tiled=True)
    return jnp.dot(
        panel,
        lax.all_gather(right_half, "gx", axis=0, tiled=True),
        preferred_element_type=jnp.float32,
    )


def shards(features, counts, ref_mean, ref_root):
    width = features.shape[1]
    slots = features.shape[0]
    rows_x = lax.axis_size("gx")
    cols_y = lax.axis_size("gy")
    tile_rows = width // rows_x
    tile_cols = width // cols_y
    keep = (jnp.arange(slots, dtype=jnp.int32) < counts[0])[:, None]
    masked = jnp.where(keep, features, jnp.zeros_like(features))
    partial_gram = lax.dot_general(
        masked, features, (((0,), (0,)), ((), ())), preferred_element_type=jnp.float32
    )
    column_total = jnp.sum(masked.astype(jnp.float32), axis=0)
    local_count = counts[0].astype(jnp.float32)
    total, count = lax.psum((column_total, local_count), ("gx", "gy"))
    column_block = lax.psum_scatter(partial_gram, "gy", scatter_dimension=1, tiled=True)
    gram_tile = lax.psum_scatter(column_block, "gx", scatter_dimension=0, tiled=True)
    mean = total / count
    row_start = lax.axis_index("gx") * tile_rows
    col_start = lax.axis_index("gy") * tile_cols
    mean_rows = lax.dynamic_slice_in_dim(mean, row_start, tile_rows, 0)
    mean_cols = lax.dynamic_slice_in_dim(mean, col_start, tile_cols, 0)
    cov_tile = (gram_tile - count * mean_rows[:, None] * mean_cols[None, :]) / (count - 1.0)
    row_ids = jnp.arange(tile_rows, dtype=jnp.int32) + row_start
    col_ids = jnp.arange(tile_cols, dtype=jnp.int32) + col_start
    identity_tile = (row_ids[:, None] == col_ids[None, :]).astype(jnp.float32)
    half = product(cov_tile, ref_root)
    prod = product(ref_root, half)
    square_sum, cov_trace, root_square = lax.psum(
        (jnp.sum(prod * prod), jnp.sum(cov_tile * identity_tile), jnp.sum(ref_root * ref_root)),
        ("gx", "gy"),
    )
    scale = jnp.sqrt(square_sum + 1.0)
    current = prod / scale
    partner = identity_tile
    for step in range(ITERS):
        middle = 1.5 * identity_tile - 0.5 * product(partner, current)
        current, partner = (product(current, middle), product(middle, partner))
    last_trace = lax.psum(jnp.sum(current * identity_tile), ("gx", "gy"))
    root = jnp.sqrt(scale) * current
    distance = (
        jnp.sum((mean - ref_mean) ** 2)
        + cov_trace
        + root_square
        - 2.0 * jnp.sqrt(scale) * last_trace
    ) / 64.0
    return (mean, root, distance)


def solution(mesh):
    return jax.shard_map(
        shards,
        mesh=mesh,
        in_specs=(P(("gx", "gy"), None), P(("gx", "gy")), P(), P("gx", "gy")),
        out_specs=(P(), P("gx", "gy"), P()),
        check_vma=False,
    )
```

profile of v0, /device:TPU:0, one launch (start us, length us, event | category | flops | bytes accessed | tf_op | source)
XLA Modules:
  0.0 1031.6 jit_solution(1172393237996310174)
XLA Ops:
  26.1 118.8 %reduce-scatter.3.cloned.1.call-done = f32[2048,256]{1,0:T(8,128)} async-done(((f32[2048,2048]{1,0:T(8,128)}), f32[2048,256]{1,0:T(8,128)}) %reduce-scatter.3.cloned.1.call-update) | async-done | bytes 2097168 | tf_op jit(solution)/shard_map/reduce_scatter | solution.py:35
  150.0 42.2 %all-reduce.1 = (f32[2048]{0:T(1024)S(1)}, f32[]{:T(128)}) all-reduce(f32[2048]{0:T(1024)S(1)} %convert_reduce_fusion, f32[]{:T(128)S(6)} %convert_element_type.69), channel_id=1, replica_groups=mesh['gx'=4,'gy'=8] {'gx','gy'}, use_global_device_ids=true, to_apply=%region_1.2 | all-reduce | flops 2049 | bytes 16392 | tf_op jit(solution)/shard_map/psum | solution.py:34
  220.6 29.8 %all-gather.27.cloned.1.call-done = bf16[512,2048]{1,0:T(8,128)(2,1)} async-done(((bf16[512,256]{1,0:T(8,128)(2,1)}), bf16[512,2048]{1,0:T(8,128)(2,1)}) %all-gather.27.cloned.1.call-update) | async-done | bytes 2097168 | tf_op jit(solution)/shard_map/all_gather | solution.py:12
  280.3 30.0 %all-gather.31.cloned.1.call-done = bf16[2048,256]{1,0:T(8,128)(2,1)} async-done(((bf16[512,256]{1,0:T(8,128)(2,1)}), bf16[2048,256]{1,0:T(8,128)(2,1)}) %all-gather.31.cloned.1.call-update) | async-done | bytes 1048592 | tf_op jit(solution)/shard_map/all_gather | solution.py:15
  313.6 40.4 %psum.44 = f32[]{:T(128)} all-reduce(f32[]{:T(128)} %get-tuple-element.15), channel_id=1, replica_groups=mesh['gx'=4,'gy'=8] {'gx','gy'}, use_global_device_ids=true, to_apply=%region_6.7 | all-reduce | flops 1 | bytes 8 | tf_op jit(solution)/shard_map/psum | solution.py:48
  355.5 27.4 %all-gather.39.cloned.1.call-done = bf16[2048,256]{0,1:T(8,128)(2,1)} async-done(((bf16[512,256]{0,1:T(8,128)(2,1)}), bf16[2048,256]{0,1:T(8,128)(2,1)}) %all-gather.39.cloned.1.call-update) | async-done | bytes 1048592 | tf_op jit(solution)/shard_map/all_gather | solution.py:15
  413.8 29.5 %all-gather.35.cloned.1.call-done = bf16[512,2048]{0,1:T(8,128)(2,1)} async-done(((bf16[512,256]{0,1:T(8,128)(2,1)}), bf16[512,2048]{0,1:T(8,128)(2,1)}) %all-gather.35.cloned.1.call-update) | async-done | bytes 2097168 | tf_op jit(solution)/shard_map/all_gather | solution.py:12
  446.7 26.2 %all-gather.47.cloned.1.call-done = bf16[2048,256]{1,0:T(8,128)(2,1)} async-done(((bf16[512,256]{1,0:T(8,128)(2,1)}), bf16[2048,256]{1,0:T(8,128)(2,1)}) %all-gather.47.cloned.1.call-update) | async-done | bytes 1048592 | tf_op jit(solution)/shard_map/all_gather | solution.py:15
  472.9 29.2 %all-gather.45.cloned.1.call-done = bf16[512,2048]{1,0:T(8,128)(2,1)} async-done(((bf16[512,256]{1,0:T(8,128)(2,1)}), bf16[512,2048]{1,0:T(8,128)(2,1)}) %all-gather.45.cloned.1.call-update) | async-done | bytes 2097168 | tf_op jit(solution)/shard_map/all_gather | solution.py:12
  506.1 26.2 %all-gather.51.cloned.1.call-done = bf16[2048,256]{1,0:T(8,128)(2,1)} async-done(((bf16[512,256]{1,0:T(8,128)(2,1)}), bf16[2048,256]{1,0:T(8,128)(2,1)}) %all-gather.51.cloned.1.call-update) | async-done | bytes 1048592 | tf_op jit(solution)/shard_map/all_gather | solution.py:15
  532.3 29.2 %all-gather.49.cloned.1.call-done = bf16[512,2048]{1,0:T(8,128)(2,1)} async-done(((bf16[512,256]{1,0:T(8,128)(2,1)}), bf16[512,2048]{1,0:T(8,128)(2,1)}) %all-gather.49.cloned.1.call-update) | async-done | bytes 2097168 | tf_op jit(solution)/shard_map/all_gather | solution.py:12
  566.1 25.9 %all-gather.43.cloned.1.call-done = bf16[512,2048]{1,0:T(8,128)(2,1)} async-done(((bf16[512,256]{1,0:T(8,128)(2,1)}), bf16[512,2048]{1,0:T(8,128)(2,1)}) %all-gather.43.cloned.1.call-update) | async-done | bytes 2097168 | tf_op jit(solution)/shard_map/all_gather | solution.py:12
  592.0 29.4 %all-gather.53.cloned.1.call-done = bf16[2048,256]{1,0:T(8,128)(2,1)} async-done(((bf16[512,256]{1,0:T(8,128)(2,1)}), bf16[2048,256]{1,0:T(8,128)(2,1)}) %all-gather.53.cloned.1.call-update) | async-done | bytes 1048592 | tf_op jit(solution)/shard_map/all_gather | solution.py:15
  650.2 29.2 %all-gather.57.cloned.1.call-done = bf16[512,2048]{1,0:T(8,128)(2,1)} async-done(((bf16[512,256]{1,0:T(8,128)(2,1)}), bf16[512,2048]{1,0:T(8,128)(2,1)}) %all-gather.57.cloned.1.call-update) | async-done | bytes 2097168 | tf_op jit(solution)/shard_map/all_gather | solution.py:12
  683.6 26.1 %all-gather.63.cloned.1.call-done = bf16[2048,256]{1,0:T(8,128)(2,1)} async-done(((bf16[512,256]{1,0:T(8,128)(2,1)}), bf16[2048,256]{1,0:T(8,128)(2,1)}) %all-gather.63.cloned.1.call-update) | async-done | bytes 1048592 | tf_op jit(solution)/shard_map/all_gather | solution.py:15
  709.6 29.2 %all-gather.61.cloned.1.call-done = bf16[512,2048]{1,0:T(8,128)(2,1)} async-done(((bf16[512,256]{1,0:T(8,128)(2,1)}), bf16[512,2048]{1,0:T(8,128)(2,1)}) %all-gather.61.cloned.1.call-update) | async-done | bytes 2097168 | tf_op jit(solution)/shard_map/all_gather | solution.py:12
  743.5 25.9 %all-gather.55.cloned.1.call-done = bf16[512,2048]{1,0:T(8,128)(2,1)} async-done(((bf16[512,256]{1,0:T(8,128)(2,1)}), bf16[512,2048]{1,0:T(8,128)(2,1)}) %all-gather.55.cloned.1.call-update) | async-done | bytes 2097168 | tf_op jit(solution)/shard_map/all_gather | solution.py:12
  769.5 29.6 %all-gather.65.cloned.1.call-done = bf16[2048,256]{1,0:T(8,128)(2,1)} async-done(((bf16[512,256]{1,0:T(8,128)(2,1)}), bf16[2048,256]{1,0:T(8,128)(2,1)}) %all-gather.65.cloned.1.call-update) | async-done | bytes 1048592 | tf_op jit(solution)/shard_map/all_gather | solution.py:15
  828.0 29.2 %all-gather.69.cloned.1.call-done = bf16[512,2048]{1,0:T(8,128)(2,1)} async-done(((bf16[512,256]{1,0:T(8,128)(2,1)}), bf16[512,2048]{1,0:T(8,128)(2,1)}) %all-gather.69.cloned.1.call-update) | async-done | bytes 2097168 | tf_op jit(solution)/shard_map/all_gather | solution.py:12
  861.2 26.2 %all-gather.75.cloned.1.call-done = bf16[2048,256]{1,0:T(8,128)(2,1)} async-done(((bf16[512,256]{1,0:T(8,128)(2,1)}), bf16[2048,256]{1,0:T(8,128)(2,1)}) %all-gather.75.cloned.1.call-update) | async-done | bytes 1048592 | tf_op jit(solution)/shard_map/all_gather | solution.py:15
  887.4 29.2 %all-gather.73.cloned.1.call-done = bf16[512,2048]{1,0:T(8,128)(2,1)} async-done(((bf16[512,256]{1,0:T(8,128)(2,1)}), bf16[512,2048]{1,0:T(8,128)(2,1)}) %all-gather.73.cloned.1.call-update) | async-done | bytes 2097168 | tf_op jit(solution)/shard_map/all_gather | solution.py:12
  920.0 27.1 %all-gather.67.cloned.1.call-done = bf16[512,2048]{1,0:T(8,128)(2,1)} async-done(((bf16[512,256]{1,0:T(8,128)(2,1)}), bf16[512,2048]{1,0:T(8,128)(2,1)}) %all-gather.67.cloned.1.call-update) | async-done | bytes 2097168 | tf_op jit(solution)/shard_map/all_gather | solution.py:12
  947.1 29.6 %all-gather.77.cloned.1.call-done = bf16[2048,256]{1,0:T(8,128)(2,1)} async-done(((bf16[512,256]{1,0:T(8,128)(2,1)}), bf16[2048,256]{1,0:T(8,128)(2,1)}) %all-gather.77.cloned.1.call-update) | async-done | bytes 1048592 | tf_op jit(solution)/shard_map/all_gather | solution.py:15
  980.7 40.4 %all-reduce = (f32[]{:T(128)}, f32[]{:T(128)}, f32[]{:T(128)}) all-reduce(f32[]{:T(128)} %get-tuple-element.4, f32[]{:T(128)} %get-tuple-element.12, f32[]{:T(128)} %get-tuple-element.3), channel_id=1, replica_groups=mesh['gx'=4,'gy'=8] {'gx','gy'}, use_global_device_ids=true, to_apply=%region_9.10 | all-reduce | flops 3 | bytes 24 | tf_op jit(solution)/shard_map/psum | solution.py:48
  (96 shorter events, 205.1 us)
Async XLA Ops:
  7.2 137.7 %reduce-scatter.3.cloned.1.call-start = ((), (), s32[]{:S(2)}) async-start(), calls=%async_computation.2 | async-start | bytes 18874368 | tf_op jit(solution)/shard_map/reduce_scatter | solution.py:35
  26.0 169.0 %reduce-scatter.5.cloned.1.call-start = ((), (), s32[]{:S(2)}) async-start(), calls=%async_computation.3 | async-start | bytes 2621440 | tf_op jit(solution)/shard_map/reduce_scatter | solution.py:36
  146.3 104.1 %all-gather.27.cloned.1.call-start = ((), (), s32[]{:S(2)}) async-start(), calls=%async_computation.4 | async-start | bytes 2359296 | tf_op jit(solution)/shard_map/all_gather | solution.py:12
  197.5 112.8 %all-gather.31.cloned.1.call-start = ((), (), s32[]{:S(2)}) async-start(), calls=%async_computation.6 | async-start | bytes 1310720 | tf_op jit(solution)/shard_map/all_gather | solution.py:15
  253.7 101.8 %all-gather.37.cloned.1.call-start = ((), (), s32[]{:S(2)}) async-start(), calls=%async_computation.9 | async-start | bytes 2359296 | tf_op jit(solution)/shard_map/all_gather | solution.py:12
  254.7 128.3 %all-gather.39.cloned.1.call-start = ((), (), s32[]{:S(2)}) async-start(), calls=%async_computation.10 | async-start | bytes 1310720 | tf_op jit(solution)/shard_map/all_gather | solution.py:15
  386.9 86.0 %all-gather.47.cloned.1.call-start = ((), (), s32[]{:S(2)}) async-start(), calls=%async_computation.14 | async-start | bytes 1310720 | tf_op jit(solution)/shard_map/all_gather | solution.py:15
  387.7 114.5 %all-gather.45.cloned.1.call-start = ((), (), s32[]{:S(2)}) async-start(), calls=%async_computation.13 | async-start | bytes 2359296 | tf_op jit(solution)/shard_map/all_gather | solution.py:12
  388.2 144.1 %all-gather.51.cloned.1.call-start = ((), (), s32[]{:S(2)}) async-start(), calls=%async_computation.16 | async-start | bytes 1310720 | tf_op jit(solution)/shard_map/all_gather | solution.py:15
  446.7 114.9 %all-gather.49.cloned.1.call-start = ((), (), s32[]{:S(2)}) async-start(), calls=%async_computation.15 | async-start | bytes 2359296 | tf_op jit(solution)/shard_map/all_gather | solution.py:12
  505.5 86.5 %all-gather.43.cloned.1.call-start = ((), (), s32[]{:S(2)}) async-start(), calls=%async_computation.12 | async-start | bytes 2359296 | tf_op jit(solution)/shard_map/all_gather | solution.py:12
  506.1 115.4 %all-gather.53.cloned.1.call-start = ((), (), s32[]{:S(2)}) async-start(), calls=%async_computation.17 | async-start | bytes 1310720 | tf_op jit(solution)/shard_map/all_gather | solution.py:15
  564.9 85.4 %all-gather.59.cloned.1.call-start = ((), (), s32[]{:S(2)}) async-start(), calls=%async_computation.20 | async-start | bytes 1310720 | tf_op jit(solution)/shard_map/all_gather | solution.py:15
  565.5 114.0 %all-gather.57.cloned.1.call-start = ((), (), s32[]{:S(2)}) async-start(), calls=%async_computation.19 | async-start | bytes 2359296 | tf_op jit(solution)/shard_map/all_gather | solution.py:12
  566.0 143.6 %all-gather.63.cloned.1.call-start = ((), (), s32[]{:S(2)}) async-start(), calls=%async_computation.22 | async-start | bytes 1310720 | tf_op jit(solution)/shard_map/all_gather | solution.py:15
  624.7 114.1 %all-gather.61.cloned.1.call-start = ((), (), s32[]{:S(2)}) async-start(), calls=%async_computation.21 | async-start | bytes 2359296 | tf_op jit(solution)/shard_map/all_gather | solution.py:12
  682.8 86.7 %all-gather.55.cloned.1.call-start = ((), (), s32[]{:S(2)}) async-start(), calls=%async_computation.18 | async-start | bytes 2359296 | tf_op jit(solution)/shard_map/all_gather | solution.py:12
  683.5 115.5 %all-gather.65.cloned.1.call-start = ((), (), s32[]{:S(2)}) async-start(), calls=%async_computation.23 | async-start | bytes 1310720 | tf_op jit(solution)/shard_map/all_gather | solution.py:15
  742.2 85.8 %all-gather.71.cloned.1.call-start = ((), (), s32[]{:S(2)}) async-start(), calls=%async_computation.26 | async-start | bytes 1310720 | tf_op jit(solution)/shard_map/all_gather | solution.py:15
  742.9 114.3 %all-gather.69.cloned.1.call-start = ((), (), s32[]{:S(2)}) async-start(), calls=%async_computation.25 | async-start | bytes 2359296 | tf_op jit(solution)/shard_map/all_gather | solution.py:12
  743.5 143.9 %all-gather.75.cloned.1.call-start = ((), (), s32[]{:S(2)}) async-start(), calls=%async_computation.28 | async-start | bytes 1310720 | tf_op jit(solution)/shard_map/all_gather | solution.py:15
  802.3 114.3 %all-gather.73.cloned.1.call-start = ((), (), s32[]{:S(2)}) async-start(), calls=%async_computation.27 | async-start | bytes 2359296 | tf_op jit(solution)/shard_map/all_gather | solution.py:12
  860.5 86.5 %all-gather.67.cloned.1.call-start = ((), (), s32[]{:S(2)}) async-start(), calls=%async_computation.24 | async-start | bytes 2359296 | tf_op jit(solution)/shard_map/all_gather | solution.py:12
  861.2 115.5 %all-gather.77.cloned.1.call-start = ((), (), s32[]{:S(2)}) async-start(), calls=%async_computation.29 | async-start | bytes 1310720 | tf_op jit(solution)/shard_map/all_gather | solution.py:15
  (8 other events, 615.0 us)
Sparse Core Ops, SparseCore 0:
  26.1 118.6 reduce-scatter.2
  147.1 44.6 reduce-scatter.4
  222.9 27.4 all-gather.26
  252.2 28.0 all-gather.32
  282.3 27.9 all-gather.30
  312.2 27.6 all-gather.36
  355.6 27.3 all-gather.38
  386.5 27.3 all-gather.40
  444.9 27.9 all-gather.46
  474.7 27.4 all-gather.44
  504.3 27.9 all-gather.50
  534.1 27.4 all-gather.48
  563.9 28.0 all-gather.42
  593.4 27.9 all-gather.52
  652.0 27.4 all-gather.56
  681.6 27.9 all-gather.62
  711.4 27.4 all-gather.60
  741.3 28.0 all-gather.54
  771.0 27.9 all-gather.64
  829.8 27.4 all-gather.68
  859.4 27.9 all-gather.74
  889.1 27.4 all-gather.72
  919.0 28.0 all-gather.66
  948.7 27.9 all-gather.76
  (4 shorter events, 108.8 us)
where the time goes:
time: 1030 us
  waiting for transfers between devices  815 us (79%)
  blocking collectives  123 us (12%)
  matrix products  61.5 us (6%)
  between operations  20.3 us (2%)
  other arithmetic  10.5 us (1%)
    all_gather x13, waiting for transfers between devices, product(): lax.all_gather(right_half, 'gx', axis=0, tiled=True)  350 us
    all_gather x13, waiting for transfers between devices, product(): panel = lax.all_gather(left_half, 'gy', axis=1, tiled=True)  339 us
    reduce_scatter x1, waiting for transfers between devices, shards(): lax.psum_scatter(partial_gram, 'gy', scatter_dimension=1, tiled=True)  119 us
    psum x2, blocking collectives, shards(): lax.psum((jnp.sum(prod * prod), jnp.sum(cov_tile * identity_tile), jnp.su...  80.7 us
    dot_general x13, matrix products, product(): jnp.dot(panel, lax.all_gather(right_half, 'gx', axis=0, tiled=True), pref...  43.4 us
    psum x1, blocking collectives, shards(): total, count = lax.psum((column_total, local_count), ('gx', 'gy'))  42.2 us
  transfers between devices with their start and end apart: 28, of which 26 were waited for; matrix products, arithmetic and copies ran while one was open for 5% of the time, Pallas kernels for 0%

commit v1 on v0

--- a/solution.py
+++ b/solution.py
@@ -9,7 +9,14 @@
 def product(left, right):
     left_half = left.astype(jnp.bfloat16)
     right_half = right.astype(jnp.bfloat16)
-    panel = lax.all_gather(left_half, "gy", axis=1, tiled=True)
+    ways = lax.axis_size("gy")
+    pieces = [left_half]
+    for far in range(1, ways):
+        pieces.append(
+            lax.ppermute(pieces[far - 1], "gy", [(d, (d - 1) % ways) for d in range(ways)])
+        )
+    line = jnp.concatenate(pieces, axis=1)
+    panel = jnp.roll(line, lax.axis_index("gy") * left_half.shape[1], axis=1)
     return jnp.dot(
         panel,
         lax.all_gather(right_half, "gx", axis=0, tiled=True),

time: 1030 us -> 805 us (0.78); the launches traced: 1030 us -> 796 us
  waiting for transfers between devices: 815 us -> 271 us
  starting transfers between devices: 1.3 us -> 240 us
  local copies, waits for them, and re-layouts: 0.09 us -> 63.1 us
    all_gather x13, waiting for transfers between devices: 350 us -> 0.13 us  [product(): lax.all_gather(right_half, 'gx', axis=0, tiled=True)]
    all_gather x13 -> x0, waiting for transfers between devices: 339 us -> none  [product(): panel = lax.all_gather(left_half, 'gy', axis=1, tiled=True)]
    ppermute x0 -> x91, starting transfers between devices: none -> 239 us  [product(): lax.ppermute(pieces[far - 1], 'gy', [(d, (d - 1) % ways) for d in range(w...]
    ppermute x0 -> x91, waiting for transfers between devices: none -> 152 us  [product(): lax.ppermute(pieces[far - 1], 'gy', [(d, (d - 1) % ways) for d in range(w...]
    unnamed x8 -> x104, local copies, waits for them, and re-layouts: 0.02 us -> 54.2 us
  transfers between devices with their start and end apart: 28 -> 106, of which waited for: 26 -> 72; matrix products, arithmetic and copies ran while one was open for 5% -> 13% of each run, Pallas kernels for 0% -> 0%
where the time goes in v1:
time: 805 us; the launch traced here: 796 us
  waiting for transfers between devices  271 us (34%)
  starting transfers between devices  240 us (30%)
  blocking collectives  123 us (15%)
  matrix products  68.8 us (9%)
  local copies, waits for them, and re-layouts  63.1 us (8%)
  between operations  20.2 us (3%)
  other arithmetic  10.4 us (1%)
    ppermute x91, starting transfers between devices, product(): lax.ppermute(pieces[far - 1], 'gy', [(d, (d - 1) % ways) for d in range(w...  239 us
    ppermute x91, waiting for transfers between devices, product(): lax.ppermute(pieces[far - 1], 'gy', [(d, (d - 1) % ways) for d in range(w...  152 us
    reduce_scatter x1, waiting for transfers between devices, shards(): lax.psum_scatter(partial_gram, 'gy', scatter_dimension=1, tiled=True)  119 us
    psum x2, blocking collectives, shards(): lax.psum((jnp.sum(prod * prod), jnp.sum(cov_tile * identity_tile), jnp.su...  80.4 us
    unnamed x104, local copies, waits for them, and re-layouts  54.2 us
    dot_general x13, matrix products, product(): jnp.dot(panel, lax.all_gather(right_half, 'gx', axis=0, tiled=True), pref...  50.8 us
    psum x1, blocking collectives, shards(): total, count = lax.psum((column_total, local_count), ('gx', 'gy'))  42.7 us
    dot_general x1, matrix products, shards(): lax.dot_general(masked, features, (((0,), (0,)), ((), ())), preferred_ele...  18.1 us
  transfers between devices with their start and end apart: 106, of which 72 were waited for; matrix products, arithmetic and copies ran while one was open for 13% of the time, Pallas kernels for 0%

profile of v1, /device:TPU:0, one launch (start us, length us, event | category | flops | bytes accessed | tf_op | source)
XLA Modules:
  0.0 796.2 jit_solution(10714754311714615748)
XLA Ops:
  7.9 18.1 %fusion = f32[2048,2048]{1,0:T(8,128)} fusion(bf16[1280,2048]{1,0:T(8,128)(2,1)} %param.6, pred[1280]{0:T(1024)(128)(4,1)S(1)} %iota_compare_fusion), kind=kOutput, calls=%fused_computation.1 | convolution fusion | flops 10740039680 | bytes 22021376 | tf_op jit(solution)/shard_map/dot_general | solution.py:36
  26.0 118.8 %reduce-scatter.3.cloned.1.call-done = f32[2048,256]{1,0:T(8,128)} async-done(((f32[2048,2048]{1,0:T(8,128)}), f32[2048,256]{1,0:T(8,128)}) %reduce-scatter.3.cloned.1.call-update) | async-done | bytes 2097168 | tf_op jit(solution)/shard_map/reduce_scatter | solution.py:42
  148.6 42.7 %all-reduce.1 = (f32[2048]{0:T(1024)S(1)}, f32[]{:T(128)}) all-reduce(f32[2048]{0:T(1024)S(1)} %convert_reduce_fusion, f32[]{:T(128)S(6)} %convert_element_type.66), channel_id=1, replica_groups=mesh['gx'=4,'gy'=8] {'gx','gy'}, use_global_device_ids=true, to_apply=%region_1.2 | all-reduce | flops 2049 | bytes 16392 | tf_op jit(solution)/shard_map/psum | solution.py:41
  197.2 3.9 collective-permute-done.7
  203.9 3.9 collective-permute-done.8
  249.3 3.9 collective-permute-done.3
  256.0 3.9 collective-permute-done.4
  279.0 40.4 %psum.44 = f32[]{:T(128)} all-reduce(f32[]{:T(128)} %get-tuple-element.20), channel_id=1, replica_groups=mesh['gx'=4,'gy'=8] {'gx','gy'}, use_global_device_ids=true, to_apply=%region_6.8 | all-reduce | flops 1 | bytes 8 | tf_op jit(solution)/shard_map/psum | solution.py:55
  322.4 3.9 collective-permute-done.21
  329.0 3.9 collective-permute-done.22
  336.1 3.9 collective-permute-done.23
  343.2 3.9 collective-permute-done.24
  448.0 3.9 collective-permute-done.45
  454.7 3.9 collective-permute-done.46
  473.5 4.4 constant_dynamic-update-slice_fusion.71
  480.9 3.9 collective-permute-done.28
  487.6 3.9 collective-permute-done.29
  557.2 3.9 collective-permute-done.63
  564.3 3.9 collective-permute-done.64
  571.4 3.9 collective-permute-done.65
  603.3 4.3 constant_dynamic-update-slice_fusion.95
  708.6 4.2 fusion.67
  741.2 4.7 fusion.102
  745.8 40.0 %all-reduce = (f32[]{:T(128)}, f32[]{:T(128)}, f32[]{:T(128)}) all-reduce(f32[]{:T(128)} %get-tuple-element.5, f32[]{:T(128)} %multiply_reduce_fusion, f32[]{:T(128)} %get-tuple-element.4), channel_id=1, replica_groups=mesh['gx'=4,'gy'=8] {'gx','gy'}, use_global_device_ids=true, to_apply=%region_9.11 | all-reduce | flops 3 | bytes 24 | tf_op jit(solution)/shard_map/psum | solution.py:55
  (350 shorter events, 440.1 us)
Async XLA Ops:
  7.2 137.6 %reduce-scatter.3.cloned.1.call-start = ((), (), s32[]{:S(2)}) async-start(), calls=%async_computation.2 | async-start | bytes 18874368 | tf_op jit(solution)/shard_map/reduce_scatter | solution.py:42
  26.0 168.1 %reduce-scatter.5.cloned.1.call-start = ((), (), s32[]{:S(2)}) async-start(), calls=%async_computation.3 | async-start | bytes 2621440 | tf_op jit(solution)/shard_map/reduce_scatter | solution.py:43
  144.8 98.1 %all-gather.14.cloned.1.call-start = ((), (), s32[]{:S(2)}) async-start(), calls=%async_computation.4 | async-start | bytes 1310720 | tf_op jit(solution)/shard_map/all_gather | solution.py:22
  211.5 63.9 %all-gather.16.cloned.1.call-start = ((), (), s32[]{:S(2)}) async-start(), calls=%async_computation.5 | async-start | bytes 1310720 | tf_op jit(solution)/shard_map/all_gather | solution.py:22
  224.1 22.4 %collective-permute-start.2 = (bf16[512,256]{1,0:T(8,128)(2,1)S(1)}, bf16[512,256]{1,0:T(8,128)(2,1)S(1)}, u32[]{:S(2)}, u32[]{:S(2)}) collective-permute-start(bf16[512,256]{1,0:T(8,128)(2,1)S(1)} %collective-permute-done.1), channel_id=1, source_target_pairs={{0,7},{1,0},{2,1},{3,2},{4,3},{5,4},{6,5},{7,6},{8,15},{9,8},{10,9... | collective-permute-start | bytes 786440 | tf_op jit(solution)/shard_map/ppermute | solution.py:16
  246.4 125.9 %all-gather.18.cloned.1.call-start = ((), (), s32[]{:S(2)}) async-start(), calls=%async_computation.6 | async-start | bytes 1310720 | tf_op jit(solution)/shard_map/all_gather | solution.py:22
  267.0 7.5 collective-permute-start.6
  321.0 99.7 %all-gather.22.cloned.1.call-start = ((), (), s32[]{:S(2)}) async-start(), calls=%async_computation.8 | async-start | bytes 1310720 | tf_op jit(solution)/shard_map/all_gather | solution.py:22
  350.4 91.0 %all-gather.20.cloned.1.call-start = ((), (), s32[]{:S(2)}) async-start(), calls=%async_computation.7 | async-start | bytes 1310720 | tf_op jit(solution)/shard_map/all_gather | solution.py:22
  403.4 25.6 %collective-permute-start.19 = (bf16[512,256]{0,1:T(8,128)(2,1)S(1)}, bf16[512,256]{0,1:T(8,128)(2,1)S(1)}, u32[]{:S(2)}, u32[]{:S(2)}) collective-permute-start(bf16[512,256]{0,1:T(8,128)(2,1)S(1)} %collective-permute-done.18), channel_id=1, source_target_pairs={{0,7},{1,0},{2,1},{3,2},{4,3},{5,4},{6,5},{7,6},{8,15},{9,8},{10,9... | collective-permute-start | bytes 786440 | tf_op jit(solution)/shard_map/ppermute | solution.py:16
  406.1 67.4 %all-gather.24.cloned.1.call-start = ((), (), s32[]{:S(2)}) async-start(), calls=%async_computation.9 | async-start | bytes 1310720 | tf_op jit(solution)/shard_map/all_gather | solution.py:22
  445.2 100.9 %all-gather.26.cloned.1.call-start = ((), (), s32[]{:S(2)}) async-start(), calls=%async_computation.10 | async-start | bytes 1310720 | tf_op jit(solution)/shard_map/all_gather | solution.py:22
  477.9 73.7 %all-gather.28.cloned.1.call-start = ((), (), s32[]{:S(2)}) async-start(), calls=%async_computation.11 | async-start | bytes 1310720 | tf_op jit(solution)/shard_map/all_gather | solution.py:22
  511.3 92.1 %all-gather.30.cloned.1.call-start = ((), (), s32[]{:S(2)}) async-start(), calls=%async_computation.12 | async-start | bytes 1310720 | tf_op jit(solution)/shard_map/all_gather | solution.py:22
  512.3 8.0 %collective-permute-start.33 = (bf16[512,256]{0,1:T(8,128)(2,1)S(1)}, bf16[512,256]{0,1:T(8,128)(2,1)S(1)}, u32[]{:S(2)}, u32[]{:S(2)}) collective-permute-start(bf16[512,256]{0,1:T(8,128)(2,1)S(1)} %collective-permute-done.32), channel_id=1, source_target_pairs={{0,7},{1,0},{2,1},{3,2},{4,3},{5,4},{6,5},{7,6},{8,15},{9,8},{10,9... | collective-permute-start | bytes 786440 | tf_op jit(solution)/shard_map/ppermute | solution.py:16
  520.4 12.0 %collective-permute-start.34 = (bf16[512,256]{0,1:T(8,128)(2,1)S(1)}, bf16[512,256]{0,1:T(8,128)(2,1)S(1)}, u32[]{:S(2)}, u32[]{:S(2)}) collective-permute-start(bf16[512,256]{0,1:T(8,128)(2,1)S(1)} %collective-permute-done.33), channel_id=1, source_target_pairs={{0,7},{1,0},{2,1},{3,2},{4,3},{5,4},{6,5},{7,6},{8,15},{9,8},{10,9... | collective-permute-start | bytes 786440 | tf_op jit(solution)/shard_map/ppermute | solution.py:16
  543.3 7.5 collective-permute-start.62
  550.0 105.6 %all-gather.34.cloned.1.call-start = ((), (), s32[]{:S(2)}) async-start(), calls=%async_computation.14 | async-start | bytes 1310720 | tf_op jit(solution)/shard_map/all_gather | solution.py:22
  585.0 25.9 %collective-permute-start.49 = (bf16[512,256]{0,1:T(8,128)(2,1)S(1)}, bf16[512,256]{0,1:T(8,128)(2,1)S(1)}, u32[]{:S(2)}, u32[]{:S(2)}) collective-permute-start(bf16[512,256]{0,1:T(8,128)(2,1)S(1)} %copy-done.8), channel_id=1, source_target_pairs={{0,7},{1,0},{2,1},{3,2},{4,3},{5,4},{6,5},{7,6},{8,15},{9,8},{10,9... | collective-permute-start | bytes 786440 | tf_op jit(solution)/shard_map/ppermute | solution.py:16
  585.0 90.8 %all-gather.32.cloned.1.call-start = ((), (), s32[]{:S(2)}) async-start(), calls=%async_computation.13 | async-start | bytes 1310720 | tf_op jit(solution)/shard_map/all_gather | solution.py:22
  638.3 25.5 %collective-permute-start.54 = (bf16[512,256]{0,1:T(8,128)(2,1)S(1)}, bf16[512,256]{0,1:T(8,128)(2,1)S(1)}, u32[]{:S(2)}, u32[]{:S(2)}) collective-permute-start(bf16[512,256]{0,1:T(8,128)(2,1)S(1)} %collective-permute-done.53), channel_id=1, source_target_pairs={{0,7},{1,0},{2,1},{3,2},{4,3},{5,4},{6,5},{7,6},{8,15},{9,8},{10,9... | collective-permute-start | bytes 786440 | tf_op jit(solution)/shard_map/ppermute | solution.py:16
  640.4 68.1 %all-gather.36.cloned.1.call-start = ((), (), s32[]{:S(2)}) async-start(), calls=%async_computation.15 | async-start | bytes 1310720 | tf_op jit(solution)/shard_map/all_gather | solution.py:22
  679.7 61.5 %all-gather.38.cloned.1.call-start = ((), (), s32[]{:S(2)}) async-start(), calls=%async_computation.16 | async-start | bytes 1310720 | tf_op jit(solution)/shard_map/all_gather | solution.py:22
  690.6 22.2 %collective-permute-start.72 = (bf16[512,256]{0,1:T(8,128)(2,1)S(1)}, bf16[512,256]{0,1:T(8,128)(2,1)S(1)}, u32[]{:S(2)}, u32[]{:S(2)}) collective-permute-start(bf16[512,256]{0,1:T(8,128)(2,1)S(1)} %collective-permute-done.71), channel_id=1, source_target_pairs={{0,7},{1,0},{2,1},{3,2},{4,3},{5,4},{6,5},{7,6},{8,15},{9,8},{10,9... | collective-permute-start | bytes 786440 | tf_op jit(solution)/shard_map/ppermute | solution.py:16
  (95 other events, 968.2 us)
Sparse Core Ops, SparseCore 0:
  26.1 118.6 reduce-scatter.2
  147.1 44.6 reduce-scatter.4
  211.6 27.0 all-gather.13
  246.5 28.8 all-gather.15
  321.1 28.4 all-gather.17
  351.0 27.3 all-gather.21
  406.3 26.5 all-gather.19
  445.3 26.4 all-gather.23
  478.1 27.9 all-gather.25
  511.4 26.4 all-gather.27
  550.2 26.0 all-gather.29
  585.1 26.0 all-gather.33
  640.6 25.9 all-gather.31
  679.8 25.9 all-gather.35
  712.9 27.8 all-gather.37
